TPU v7x, 32 devices: a whole 2x2x4 slice. The times are simulated.
32 devices in a mesh: lat: 4 (over y, x), ord: 4 (over z), batch: 2 (over core).
Axes of the slice: x: 2, y: 2, z: 4, core: 2. Of those that a mesh axis runs over, the one named last changes fastest.
Arguments:
- state_field: bfloat16 [512, 720, 1440], P(('batch', 'ord'), 'lat'), parts along dimension 0, may hold values from -6 to 6
- slot_order: int32 [512], replicated, may hold values from 0 to 511, each once
- legendre: bfloat16 [512, 720, 720], P(('lat', 'ord')), may hold values from -0.21875 to 0.21875
- degree_gain: float32 [720, 256], replicated, may hold values from 0.25 to 1.75
- mixing: bfloat16 [256, 256], replicated, may hold values from -0.375 to 0.375
Outputs:
- updated: bfloat16 [512, 720, 1440], P(('batch', 'ord'), 'lat'), parts along dimension 0
There are 2 independent parts, one for each index of `batch`. A program takes and returns all parts, laid end to end along the dimension named above; an argument that names none is the same for every part. Nothing has to cross between parts.
Inputs may be any that keep to these rules, and one draw needn't show every extreme that they name: `slot_order`: each of 0 to 511 stands once.
All inputs are finite; a program needn't handle non-finite values.
Results may differ from a plain program's by a relative error of at most 0.0054.
Values may be sent and summed in bfloat16 or wider, within the bound.
A program may use at most 320 MiB of HBM per device.

v0:
```python
import functools
import math

import jax
import jax.numpy as jnp
from jax import lax
from jax.experimental import pallas as pl
from jax.experimental.pallas import tpu as pltpu
from jax.sharding import PartitionSpec as P

CHUNKS = 4


def table(orders, lon_count):
    longitude = lax.broadcasted_iota(jnp.int32, orders.shape + (lon_count,), orders.ndim)
    product = (orders[..., None] * longitude).astype(jnp.float32)
    turns = jnp.floor((product + 0.5) * (1.0 / lon_count))
    angle = (product - turns * lon_count) * (2.0 * math.pi / lon_count)
    root = 1.0 / math.sqrt(lon_count)
    return (jnp.cos(angle) * root).astype(jnp.bfloat16), (-jnp.sin(angle) * root).astype(jnp.bfloat16)


def middle_kernel(orders_ref, coeffs_ref, legendre_ref, gain_ref, mixing_ref, out_ref):
    order = orders_ref[pl.program_id(0)]
    slot_table = legendre_ref[0]
    mixing = mixing_ref[...]
    degrees = slot_table.shape[0]
    width = mixing.shape[0]
    weight = jnp.where(order == 0, 1.0, 2.0).astype(jnp.float32)
    kept = lax.broadcasted_iota(jnp.int32, (degrees, width), 0) < degrees - order
    start = pl.multiple_of(order // 8 * 8, 8)
    window = gain_ref[pl.ds(start, degrees + 8), :]
    gain = pltpu.roll(window, degrees + 8 - order % 8, 0)[:degrees]
    for part in range(2):
        spec = lax.dot_general(
            slot_table, coeffs_ref[0, part], (((1,), (0,)), ((), ())), preferred_element_type=jnp.float32
        )
        filtered = jnp.where(kept, spec * gain, 0.0).astype(jnp.bfloat16)
        mixed = jnp.dot(filtered, mixing, preferred_element_type=jnp.float32).astype(jnp.bfloat16)
        synth = lax.dot_general(
            slot_table, mixed, (((0,), (0,)), ((), ())), preferred_element_type=jnp.float32
        )
        out_ref[0, part] = (synth * weight).astype(jnp.bfloat16)


def middle(orders, coeffs, legendre, first, padded_gain, mixing):
    slots, parts, latitudes, width = coeffs.shape
    degrees = legendre.shape[1]
    return pl.pallas_call(
        middle_kernel,
        out_shape=jax.ShapeDtypeStruct(coeffs.shape, jnp.bfloat16),
        grid_spec=pltpu.PrefetchScalarGridSpec(
            num_scalar_prefetch=1,
            grid=(slots,),
            in_specs=[
                pl.BlockSpec((1, parts, latitudes, width), lambda s, o: (s, 0, 0, 0)),
                pl.BlockSpec((1, degrees, latitudes), lambda s, o: (first + s, 0, 0)),
                pl.BlockSpec(padded_gain.shape, lambda s, o: (0, 0)),
                pl.BlockSpec(mixing.shape, lambda s, o: (0, 0)),
            ],
            out_specs=pl.BlockSpec((1, parts, latitudes, width), lambda s, o: (s, 0, 0, 0)),
        ),
        compiler_params=pltpu.CompilerParams(vmem_limit_bytes=40 * 1024 * 1024),
        cost_estimate=pl.CostEstimate(
            flops=2 * slots * parts * width * degrees * (2 * latitudes + width),
            bytes_accessed=2 * slots * latitudes * (2 * parts * width + degrees),
            transcendentals=0,
        ),
    )(orders, coeffs, legendre, padded_gain, mixing)


def shards(state_field, slot_order, legendre, degree_gain, mixing):
    channels, lat_rows, lon_count = state_field.shape
    all_slots = slot_order.shape[0]
    my_slots, degrees, latitudes = legendre.shape
    width = mixing.shape[0]
    lat_count = lax.axis_size("lat")
    ord_count = lax.axis_size("ord")
    devices = lat_count * ord_count
    chunks = math.gcd(CHUNKS, my_slots)
    piece = my_slots // chunks
    rows = channels * lat_rows
    me = lax.axis_index(("lat", "ord"))
    grid_rows = state_field.transpose(1, 0, 2).reshape(rows, lon_count)
    orders_by_device = slot_order.reshape(devices, chunks, piece)
    padded_gain = jnp.concatenate([degree_gain, jnp.zeros((degrees + 8, width), jnp.float32)], axis=0)

    tables = []
    arrived = []
    for g in range(chunks):
        cosine, sine = table(orders_by_device[:, g], lon_count)
        rows_here = jnp.stack([cosine, sine], axis=1).reshape(2 * devices * piece, lon_count)
        tables.append(rows_here)
        fourier = lax.dot_general(
            rows_here, grid_rows, (((1,), (1,)), ((), ())), preferred_element_type=jnp.float32
        ).astype(jnp.bfloat16)
        arrived.append(
            lax.all_to_all(
                fourier.reshape(devices, 2 * piece, rows),
                ("lat", "ord"),
                split_axis=0,
                concat_axis=0,
                tiled=True,
            )
        )

    returned = []
    for g in range(chunks):
        coeffs = arrived[g].reshape(lat_count, ord_count, 2, piece, lat_rows, channels)
        coeffs = coeffs.transpose(3, 2, 0, 4, 1, 5).reshape(piece, 2, latitudes, width)
        orders_here = lax.dynamic_slice_in_dim(slot_order, me * my_slots + g * piece, piece, 0)
        synth = middle(orders_here, coeffs, legendre, g * piece, padded_gain, mixing)
        outgoing = synth.reshape(piece, 2, lat_count, lat_rows, ord_count, channels)
        outgoing = outgoing.transpose(2, 4, 1, 0, 3, 5).reshape(devices, 2 * piece, rows)
        returned.append(
            lax.all_to_all(outgoing, ("lat", "ord"), split_axis=0, concat_axis=0, tiled=True).reshape(
                2 * devices * piece, rows
            )
        )

    back = lax.dot_general(
        jnp.concatenate(returned, axis=0),
        jnp.concatenate(tables, axis=0),
        (((0,), (0,)), ((), ())),
        preferred_element_type=jnp.float32,
    )
    back = back.reshape(lat_rows, channels, lon_count).transpose(1, 0, 2)
    return (state_field.astype(jnp.float32) + jax.nn.gelu(back, approximate=True)).astype(
        jnp.bfloat16
    )


def solution(mesh):
    placed = (P(("batch", "ord"), "lat", None), P(), P(("lat", "ord"), None, None), P(), P())
    return jax.shard_map(
        shards,
        mesh=mesh,
        in_specs=placed,
        out_specs=P(("batch", "ord"), "lat", None),
        check_vma=False,
    )
```

profile of v0, /device:TPU:0, one launch (start us, length us, event | category | flops | bytes accessed | tf_op | source)
XLA Modules:
  0.0 1297.0 jit_solution(8171077813688594166)
XLA Ops:
  4.3 18.2 %convolution_convert_fusion.2 = bf16[256,11520]{1,0:T(8,128)(2,1)} fusion(bf16[256,1440]{1,0:T(8,128)(2,1)S(1)} %bitcast.71, bf16[11520,1440]{1,0:T(8,128)(2,1)} %bitcast.58), kind=kOutput, calls=%fused_computation.20 | convolution fusion | flops 8496414720 | bytes 39813120 | tf_op jit(solution)/shard_map/dot_general | solution.py:94
  34.4 18.3 %convolution_convert_fusion.1 = bf16[256,11520]{1,0:T(8,128)(2,1)} fusion(bf16[256,1440]{1,0:T(8,128)(2,1)S(1)} %bitcast.73, bf16[11520,1440]{1,0:T(8,128)(2,1)} %bitcast.59), kind=kOutput, calls=%fused_computation.19 | convolution fusion | flops 8496414720 | bytes 39813120 | tf_op jit(solution)/shard_map/dot_general | solution.py:94
  52.6 118.0 %all-to-all-done.2 = bf16[16,16,11520]{2,1,0:T(8,128)(2,1)} async-done(((bf16[16,16,11520]{2,1,0:T(8,128)(2,1)}), bf16[16,16,11520]{2,1,0:T(8,128)(2,1)}, u32[]{:S(2)}, u32[]{:S(2)}) %all-to-all-start.2) | async-done | bytes 5898272 | tf_op jit(solution)/shard_map/all_to_all | solution.py:98
  178.7 18.2 %convolution_convert_fusion = bf16[256,11520]{1,0:T(8,128)(2,1)} fusion(bf16[256,1440]{1,0:T(8,128)(2,1)S(1)} %bitcast.75, bf16[11520,1440]{1,0:T(8,128)(2,1)} %bitcast.60), kind=kOutput, calls=%fused_computation.18 | convolution fusion | flops 8496414720 | bytes 39813120 | tf_op jit(solution)/shard_map/dot_general | solution.py:94
  196.9 120.4 %all-to-all-done.4 = bf16[16,16,11520]{2,1,0:T(8,128)(2,1)} async-done(((bf16[16,16,11520]{2,1,0:T(8,128)(2,1)}), bf16[16,16,11520]{2,1,0:T(8,128)(2,1)}, u32[]{:S(2)}, u32[]{:S(2)}) %all-to-all-start.4) | async-done | bytes 5898272 | tf_op jit(solution)/shard_map/all_to_all | solution.py:98
  325.6 18.2 %convolution_convert_fusion.3 = bf16[256,11520]{1,0:T(8,128)(2,1)} fusion(bf16[256,1440]{1,0:T(8,128)(2,1)S(1)} %bitcast.77, bf16[11520,1440]{1,0:T(8,128)(2,1)} %bitcast.61), kind=kOutput, calls=%fused_computation.21 | convolution fusion | flops 8496414720 | bytes 39813120 | tf_op jit(solution)/shard_map/dot_general | solution.py:94
  343.9 120.1 %all-to-all-done.6 = bf16[16,16,11520]{2,1,0:T(8,128)(2,1)} async-done(((bf16[16,16,11520]{2,1,0:T(8,128)(2,1)}), bf16[16,16,11520]{2,1,0:T(8,128)(2,1)}, u32[]{:S(2)}, u32[]{:S(2)}) %all-to-all-start.6) | async-done | bytes 5898272 | tf_op jit(solution)/shard_map/all_to_all | solution.py:98
  484.5 22.9 %copy.44 = bf16[8,2,4,180,4,64]{5,4,3,2,1,0:T(4,128)(2,1)} copy(bf16[8,2,4,180,4,64]{5,3,0,1,4,2:T(8,128)(2,1)} %bitcast.54) | data formatting | bytes 11796480 | tf_op jit(solution)/shard_map/reshape | solution.py:110
  527.6 21.9 %shard_map.58 = bf16[8,2,720,256]{3,2,1,0:T(8,128)(2,1)S(1)} custom-call(s32[8]{0:T(128)S(1)} %get-tuple-element.19.orders_ref, bf16[8,2,720,256]{3,2,1,0:T(8,128)(2,1)S(1)} %copy-done.2, bf16[32,720,720]{2,1,0:T(8,128)(2,1)} %legendre_ref.7, f32[1448,256]{1,0:T(8,128)S(1)} %concatenate.9.gain_ref, bf16[256,256]{1,0:T(8,128)(2,1)S(1)} %copy-done.8), custom_call_target="tpu_custom_call" | custom-call | flops 10003415040 | bytes 20090880 | tf_op jit(solution)/shard_map/pallas_call | solution.py:49
  578.5 18.9 %copy.34 = bf16[4,4,2,8,180,64]{5,4,3,2,1,0:T(8,128)(2,1)} copy(bf16[4,4,2,8,180,64]{4,0,5,1,2,3:T(4,128)(2,1)} %bitcast.62) | data formatting | bytes 11796480 | tf_op jit(solution)/shard_map/transpose | solution.py:114
  635.9 22.9 %copy.38 = bf16[8,2,4,180,4,64]{5,4,3,2,1,0:T(4,128)(2,1)} copy(bf16[8,2,4,180,4,64]{5,3,0,1,4,2:T(8,128)(2,1)} %bitcast.55) | data formatting | bytes 11796480 | tf_op jit(solution)/shard_map/reshape | solution.py:110
  678.9 21.9 %shard_map.55 = bf16[8,2,720,256]{3,2,1,0:T(8,128)(2,1)S(1)} custom-call(s32[8]{0:T(128)S(1)} %get-tuple-element.17.orders_ref, bf16[8,2,720,256]{3,2,1,0:T(8,128)(2,1)S(1)} %copy-done.4, bf16[32,720,720]{2,1,0:T(8,128)(2,1)} %legendre_ref.7, f32[1448,256]{1,0:T(8,128)S(1)} %concatenate.9.gain_ref, bf16[256,256]{1,0:T(8,128)(2,1)S(1)} %copy-done.8), custom_call_target="tpu_custom_call" | custom-call | flops 10003415040 | bytes 20090880 | tf_op jit(solution)/shard_map/pallas_call | solution.py:49
  729.9 18.9 %copy.16 = bf16[4,4,2,8,180,64]{5,4,3,2,1,0:T(8,128)(2,1)} copy(bf16[4,4,2,8,180,64]{4,0,5,1,2,3:T(4,128)(2,1)} %bitcast.63) | data formatting | bytes 11796480 | tf_op jit(solution)/shard_map/transpose | solution.py:114
  787.2 22.9 %copy.42 = bf16[8,2,4,180,4,64]{5,4,3,2,1,0:T(4,128)(2,1)} copy(bf16[8,2,4,180,4,64]{5,3,0,1,4,2:T(8,128)(2,1)} %bitcast.56) | data formatting | bytes 11796480 | tf_op jit(solution)/shard_map/reshape | solution.py:110
  830.2 21.9 %shard_map.57 = bf16[8,2,720,256]{3,2,1,0:T(8,128)(2,1)S(1)} custom-call(s32[8]{0:T(128)S(1)} %get-tuple-element.20.orders_ref, bf16[8,2,720,256]{3,2,1,0:T(8,128)(2,1)S(1)} %copy-done.6, bf16[32,720,720]{2,1,0:T(8,128)(2,1)} %legendre_ref.7, f32[1448,256]{1,0:T(8,128)S(1)} %concatenate.9.gain_ref, bf16[256,256]{1,0:T(8,128)(2,1)S(1)} %copy-done.8), custom_call_target="tpu_custom_call" | custom-call | flops 10003415040 | bytes 20090880 | tf_op jit(solution)/shard_map/pallas_call | solution.py:49
  863.1 18.1 %reshape.317 = bf16[8,2,4,180,4,64]{3,2,5,4,1,0:T(4,128)(2,1)} reshape(bf16[8,2,720,256]{2,3,1,0:T(8,128)(2,1)} %copy.27) | data formatting | bytes 11796480 | tf_op jit(solution)/shard_map/reshape | solution.py:113
  881.1 18.9 %copy.28 = bf16[4,4,2,8,180,64]{5,4,3,2,1,0:T(8,128)(2,1)} copy(bf16[4,4,2,8,180,64]{4,0,5,1,2,3:T(4,128)(2,1)} %bitcast.64) | data formatting | bytes 11796480 | tf_op jit(solution)/shard_map/transpose | solution.py:114
  938.5 22.9 %copy.40 = bf16[8,2,4,180,4,64]{5,4,3,2,1,0:T(4,128)(2,1)} copy(bf16[8,2,4,180,4,64]{5,3,0,1,4,2:T(8,128)(2,1)} %bitcast.57) | data formatting | bytes 11796480 | tf_op jit(solution)/shard_map/reshape | solution.py:110
  981.5 21.9 %shard_map.56 = bf16[8,2,720,256]{3,2,1,0:T(8,128)(2,1)S(1)} custom-call(s32[8]{0:T(128)S(1)} %get-tuple-element.18.orders_ref, bf16[8,2,720,256]{3,2,1,0:T(8,128)(2,1)S(1)} %copy-done, bf16[32,720,720]{2,1,0:T(8,128)(2,1)} %legendre_ref.7, f32[1448,256]{1,0:T(8,128)S(1)} %concatenate.9.gain_ref, bf16[256,256]{1,0:T(8,128)(2,1)S(1)} %copy-done.8), custom_call_target="tpu_custom_call" | custom-call | flops 10003415040 | bytes 20090880 | tf_op jit(solution)/shard_map/pallas_call | solution.py:49
  1014.4 18.1 %reshape.310 = bf16[8,2,4,180,4,64]{3,2,5,4,1,0:T(4,128)(2,1)} reshape(bf16[8,2,720,256]{2,3,1,0:T(8,128)(2,1)} %copy.21) | data formatting | bytes 11796480 | tf_op jit(solution)/shard_map/reshape | solution.py:113
  1032.4 18.9 %copy.22 = bf16[4,4,2,8,180,64]{5,4,3,2,1,0:T(8,128)(2,1)} copy(bf16[4,4,2,8,180,64]{4,0,5,1,2,3:T(4,128)(2,1)} %bitcast.65) | data formatting | bytes 11796480 | tf_op jit(solution)/shard_map/transpose | solution.py:114
  1069.9 135.8 %all_to_all.40 = bf16[16,16,11520]{2,1,0:T(8,128)(2,1)} all-to-all(bf16[16,16,11520]{2,1,0:T(8,128)(2,1)} %reshape.311), channel_id=1, replica_groups=mesh['lat'=4,'ord'=4,'batch'=2] {'lat','ord'}, dimensions={0} | all-to-all | bytes 11796480 | tf_op jit(solution)/shard_map/all_to_all | solution.py:116
  1205.7 45.2 %fusion.9 = f32[11520,1440]{1,0:T(8,128)} fusion(bf16[256,11520]{1,0:T(8,128)(2,1)} %bitcast.26, bf16[256,11520]{1,0:T(8,128)(2,1)} %bitcast.20, bf16[256,11520]{1,0:T(8,128)(2,1)} %bitcast.70, bf16[256,11520]{1,0:T(8,128)(2,1)} %bitcast.7, bf16[256,1440]{1,0:T(8,128)(2,1)S(1)} %bitcast.76, bf16[256,1440]{1,0:T(8,128)(2,1)S(1)} %bitcast.74, ...), kind=kOutput, calls=%fused_computation.10 | convolution fusion | flops 34080030720 | bytes 92897280 | tf_op jit(solution)/shard_map/dot_general | solution.py:121
  1250.9 45.6 %fusion.8 = bf16[64,180,1440]{2,0,1:T(8,128)(2,1)} fusion(f32[64,180,1440]{2,0,1:T(8,128)} %bitcast.28, bf16[64,180,1440]{2,0,1:T(8,128)(2,1)} %param.5), kind=kLoop, calls=%fused_computation.9 | loop fusion | flops 182476800 | bytes 132710400 | tf_op jit(solution)/shard_map/convert_element_type | solution.py:128
  (79 shorter events, 347.5 us)
Async XLA Ops:
  4.3 18.2 %copy-start.9 = (bf16[16,2,8,1440]{3,2,1,0:T(8,128)(2,1)}, bf16[16,2,8,1440]{3,2,1,0:T(8,128)(2,1)S(1)}, u32[]{:S(2)}) copy-start(bf16[16,2,8,1440]{3,2,1,0:T(8,128)(2,1)S(1)} %pad_maximum_fusion.1) | copy-start | bytes 2211844
  22.5 148.1 %all-to-all-start.2 = ((bf16[16,16,11520]{2,1,0:T(8,128)(2,1)}), bf16[16,16,11520]{2,1,0:T(8,128)(2,1)}, u32[]{:S(2)}, u32[]{:S(2)}) async-start(bf16[16,16,11520]{2,1,0:T(8,128)(2,1)} %bitcast.69), calls=%async_computation.2 | async-start | bytes 11796480 | tf_op jit(solution)/shard_map/all_to_all | solution.py:98
  34.3 18.3 %copy-start.11 = (bf16[16,2,8,1440]{3,2,1,0:T(8,128)(2,1)}, bf16[16,2,8,1440]{3,2,1,0:T(8,128)(2,1)S(1)}, u32[]{:S(2)}) copy-start(bf16[16,2,8,1440]{3,2,1,0:T(8,128)(2,1)S(1)} %pad_maximum_fusion.2) | copy-start | bytes 2211844
  170.6 146.7 %all-to-all-start.4 = ((bf16[16,16,11520]{2,1,0:T(8,128)(2,1)}), bf16[16,16,11520]{2,1,0:T(8,128)(2,1)}, u32[]{:S(2)}, u32[]{:S(2)}) async-start(bf16[16,16,11520]{2,1,0:T(8,128)(2,1)} %bitcast.68), calls=%async_computation.4 | async-start | bytes 11796480 | tf_op jit(solution)/shard_map/all_to_all | solution.py:98
  178.7 18.2 %copy-start.13 = (bf16[16,2,8,1440]{3,2,1,0:T(8,128)(2,1)}, bf16[16,2,8,1440]{3,2,1,0:T(8,128)(2,1)S(1)}, u32[]{:S(2)}) copy-start(bf16[16,2,8,1440]{3,2,1,0:T(8,128)(2,1)S(1)} %pad_maximum_fusion.3) | copy-start | bytes 2211844
  317.3 146.7 %all-to-all-start.6 = ((bf16[16,16,11520]{2,1,0:T(8,128)(2,1)}), bf16[16,16,11520]{2,1,0:T(8,128)(2,1)}, u32[]{:S(2)}, u32[]{:S(2)}) async-start(bf16[16,16,11520]{2,1,0:T(8,128)(2,1)} %bitcast.67), calls=%async_computation.6 | async-start | bytes 11796480 | tf_op jit(solution)/shard_map/all_to_all | solution.py:98
  325.6 18.3 %copy-start.15 = (bf16[16,2,8,1440]{3,2,1,0:T(8,128)(2,1)}, bf16[16,2,8,1440]{3,2,1,0:T(8,128)(2,1)S(1)}, u32[]{:S(2)}) copy-start(bf16[16,2,8,1440]{3,2,1,0:T(8,128)(2,1)S(1)} %pad_maximum_fusion) | copy-start | bytes 2211844
  343.8 124.8 %copy-start.17 = (f32[720,256]{1,0:T(8,128)S(1)}, f32[720,256]{1,0:T(8,128)}, u32[]{:S(2)}) copy-start(f32[720,256]{1,0:T(8,128)} %param.8) | copy-start | bytes 2211844
  343.9 124.9 %copy-start.18 = (s32[512]{0:T(512)S(1)}, s32[512]{0:T(512)}, u32[]{:S(2)}) copy-start(s32[512]{0:T(512)} %param.6) | copy-start | bytes 6148
  464.0 148.9 %all-to-all-start = ((bf16[16,16,11520]{2,1,0:T(8,128)(2,1)}), bf16[16,16,11520]{2,1,0:T(8,128)(2,1)}, u32[]{:S(2)}, u32[]{:S(2)}) async-start(bf16[16,16,11520]{2,1,0:T(8,128)(2,1)} %bitcast.66), calls=%async_computation | async-start | bytes 11796480 | tf_op jit(solution)/shard_map/all_to_all | solution.py:98
  507.4 17.5 %copy-start.8 = (bf16[256,256]{1,0:T(8,128)(2,1)S(1)}, bf16[256,256]{1,0:T(8,128)(2,1)}, u32[]{:S(2)}) copy-start(bf16[256,256]{1,0:T(8,128)(2,1)} %mixing_ref.7) | copy-start | bytes 393220
  524.9 2.7 copy-start.2
  612.9 153.5 %all-to-all-start.7 = ((bf16[16,16,11520]{2,1,0:T(8,128)(2,1)}), bf16[16,16,11520]{2,1,0:T(8,128)(2,1)}, u32[]{:S(2)}, u32[]{:S(2)}) async-start(bf16[16,16,11520]{2,1,0:T(8,128)(2,1)} %reshape.325), calls=%async_computation.7 | async-start | bytes 11796480 | tf_op jit(solution)/shard_map/all_to_all | solution.py:116
  676.3 2.7 copy-start.4
  700.8 2.6 copy-start.5
  766.4 150.6 %all-to-all-start.1 = ((bf16[16,16,11520]{2,1,0:T(8,128)(2,1)}), bf16[16,16,11520]{2,1,0:T(8,128)(2,1)}, u32[]{:S(2)}, u32[]{:S(2)}) async-start(bf16[16,16,11520]{2,1,0:T(8,128)(2,1)} %reshape.304), calls=%async_computation.1 | async-start | bytes 11796480 | tf_op jit(solution)/shard_map/all_to_all | solution.py:116
  827.6 2.7 copy-start.6
  917.0 152.9 %all-to-all-start.5 = ((bf16[16,16,11520]{2,1,0:T(8,128)(2,1)}), bf16[16,16,11520]{2,1,0:T(8,128)(2,1)}, u32[]{:S(2)}, u32[]{:S(2)}) async-start(bf16[16,16,11520]{2,1,0:T(8,128)(2,1)} %reshape.318), calls=%async_computation.5 | async-start | bytes 11796480 | tf_op jit(solution)/shard_map/all_to_all | solution.py:116
  978.9 2.7 copy-start
  1003.4 2.5 copy-start.1
  1051.3 154.3 %copy-start.10 = (bf16[16,2,8,1440]{3,2,1,0:T(8,128)(2,1)S(1)}, bf16[16,2,8,1440]{3,2,1,0:T(8,128)(2,1)}, u32[]{:S(2)}) copy-start(bf16[16,2,8,1440]{3,2,1,0:T(8,128)(2,1)} %copy-done.9) | copy-start | bytes 2211844
  1051.3 154.3 %copy-start.12 = (bf16[16,2,8,1440]{3,2,1,0:T(8,128)(2,1)S(1)}, bf16[16,2,8,1440]{3,2,1,0:T(8,128)(2,1)}, u32[]{:S(2)}) copy-start(bf16[16,2,8,1440]{3,2,1,0:T(8,128)(2,1)} %copy-done.11) | copy-start | bytes 2211844
  1051.3 154.3 %copy-start.14 = (bf16[16,2,8,1440]{3,2,1,0:T(8,128)(2,1)S(1)}, bf16[16,2,8,1440]{3,2,1,0:T(8,128)(2,1)}, u32[]{:S(2)}) copy-start(bf16[16,2,8,1440]{3,2,1,0:T(8,128)(2,1)} %copy-done.13) | copy-start | bytes 2211844
  1051.4 154.3 %copy-start.16 = (bf16[16,2,8,1440]{3,2,1,0:T(8,128)(2,1)S(1)}, bf16[16,2,8,1440]{3,2,1,0:T(8,128)(2,1)}, u32[]{:S(2)}) copy-start(bf16[16,2,8,1440]{3,2,1,0:T(8,128)(2,1)} %copy-done.15) | copy-start | bytes 2211844
  (2 other events, 5.0 us)
where the time goes:
time: 1310 us; the launch traced here: 1300 us
  local copies, waits for them, and re-layouts  490 us (37%)
  waiting for transfers between devices  365 us (28%)
  blocking collectives  136 us (10%)
  matrix products  118 us (9%)
  Pallas kernels  87.5 us (7%)
  other arithmetic  59.4 us (5%)
  starting transfers between devices  40.6 us (3%)
    all_to_all x4, waiting for transfers between devices, shards(): lax.all_to_all(fourier.reshape(devices, 2 * piece, rows), ('lat', 'ord'),...  358 us
    reshape x8, local copies, waits for them, and re-layouts, shards(): coeffs.transpose(3, 2, 0, 4, 1, 5).reshape(piece, 2, latitudes, width)  162 us
    all_to_all x1, blocking collectives, shards(): lax.all_to_all(outgoing, ('lat', 'ord'), split_axis=0, concat_axis=0, til...  136 us
    pallas_call x4, Pallas kernels, middle(): pl.pallas_call(middle_kernel, out_shape=jax.ShapeDtypeStruct(coeffs.shape...  87.5 us
    transpose x4, local copies, waits for them, and re-layouts, shards(): outgoing.transpose(2, 4, 1, 0, 3, 5).reshape(devices, 2 * piece, rows)  75.6 us
    dot_general x4, matrix products, shards(): lax.dot_general(rows_here, grid_rows, (((1,), (1,)), ((), ())), preferred...  72.9 us
    reshape x4, local copies, waits for them, and re-layouts, shards(): outgoing = synth.reshape(piece, 2, lat_count, lat_rows, ord_count, channels)  72.3 us
    reshape x4, local copies, waits for them, and re-layouts, shards(): arrived[g].reshape(lat_count, ord_count, 2, piece, lat_rows, channels)  62.8 us
  transfers between devices with their start and end apart: 7, of which 6 were waited for; matrix products, arithmetic and copies ran while one was open for 41% of the time, Pallas kernels for 7%

commit v1 on v0

--- a/solution.py
+++ b/solution.py
@@ -69,7 +69,7 @@
     )(orders, coeffs, legendre, padded_gain, mixing)
 
 
-def shards(state_field, slot_order, legendre, degree_gain, mixing):
+def plain_shards(state_field, slot_order, legendre, degree_gain, mixing):
     channels, lat_rows, lon_count = state_field.shape
     all_slots = slot_order.shape[0]
     my_slots, degrees, latitudes = legendre.shape
@@ -130,12 +130,467 @@
     )
 
 
+MESH = pl.DeviceIdType.MESH
+GROUP = 8
+TILE = 15
+BLOCK = 5
+
+
+def order_of_sends(lat_count, ord_count):
+    steps = sorted(range(ord_count), key=lambda dz: (dz == 0, abs(2 * dz - ord_count)))
+    return [(dl, dz) for dz in steps for dl in range(lat_count) if (dl, dz) != (0, 0)]
+
+
+def cuts_of(tiles):
+    counts = [2] * ((tiles - 2) // 2) + [1] * (tiles % 2 + 2)
+    return [(sum(counts[:k]), count) for k, count in enumerate(counts)]
+
+
+def cosine(phase, lon_count):
+    turns = jnp.floor((phase + 0.5) * (1.0 / lon_count))
+    fold = jnp.abs(phase - turns * lon_count - lon_count // 2) - lon_count // 4
+    angle = fold * (2.0 * math.pi / lon_count)
+    square = angle * angle
+    series = 1.0 / math.factorial(13)
+    for n in (11, 9, 7, 5, 3, 1):
+        series = series * square + (-1.0) ** (n // 2) / math.factorial(n)
+    return series * angle
+
+
+def whole_kernel(
+    sizes, x_ref, rows_ref, legendre_ref, degree_gain_ref, mixing_ref,
+    out_ref, fs_ref, cb_ref, ys_ref, yb_ref,
+    table_ref, gains, xv, stage, av, z, legv, rhs, v,
+    gain_sem, x_sem, stage_sem, a_sem, leg_sem, v_sem, o_sem, own_sem,
+    send_f, recv_f, send_r, recv_r, recv_last,
+):
+    lat_count, ord_count, groups, half, channels, slots = sizes
+    devices = lat_count * ord_count
+    lanes = 2 * channels
+    pair_rows = 2 * GROUP
+    width = ord_count * channels
+    degrees = legendre_ref.shape[1]
+    order_bits = (devices * slots - 1).bit_length()
+    lon_count = x_ref.shape[2]
+    tiles = half // TILE
+    la = lax.axis_index("lat")
+    oz = lax.axis_index("ord")
+    bt = lax.axis_index("batch")
+    first_slot = (la * ord_count + oz) * slots
+    sends = order_of_sends(lat_count, ord_count)
+    cuts = cuts_of(tiles)
+
+    def ahead(dl, dz):
+        return ((la + dl) % lat_count, (oz + dz) % ord_count, bt)
+
+    def behind(dl, dz):
+        return ((la + (lat_count - dl)) % lat_count, (oz + (ord_count - dz)) % ord_count, bt)
+
+    def x_copies(tile, slot):
+        return [
+            pltpu.make_async_copy(
+                x_ref.at[pl.ds(h * half + tile * TILE, TILE)], xv.at[slot, :, h], x_sem.at[slot, h]
+            )
+            for h in range(2)
+        ]
+
+    def leg_copy(q, slot):
+        return pltpu.make_async_copy(legendre_ref.at[q], legv.at[slot], leg_sem.at[slot])
+
+    for c in x_copies(0, 0):
+        c.start()
+    leg_copy(0, 0).start()
+    gain_copy = pltpu.make_async_copy(degree_gain_ref, gains.at[pl.ds(0, degrees)], gain_sem)
+    gain_copy.start()
+    gains[degrees:, :] = jnp.zeros((gains.shape[0] - degrees, width), jnp.float32)
+
+    barrier = pltpu.get_barrier_semaphore()
+    for dl, dz in sends:
+        pl.semaphore_signal(barrier, inc=1, device_id=ahead(dl, dz), device_id_type=MESH)
+    pl.semaphore_wait(barrier, devices - 1)
+
+    def send(src, dst, part, dest, ssem, rsem):
+        pltpu.make_async_remote_copy(
+            src_ref=src.at[part], dst_ref=dst.at[part], send_sem=ssem, recv_sem=rsem,
+            device_id=dest, device_id_type=MESH,
+        ).start()
+
+    def send_forward(g):
+        for dl, dz in sends:
+            part = (g, dl * ord_count + dz)
+            send(fs_ref, cb_ref, part, ahead(dl, dz), send_f.at[g], recv_f.at[g])
+
+    def send_back(g):
+        for dl, dz in sends:
+            part = (g, dl * ord_count + dz)
+            send(ys_ref, yb_ref, part, behind(dl, dz), send_r.at[g], recv_r.at[g])
+
+    def table_block(g, k):
+        here = pl.ds(pl.multiple_of((g * devices + k) * pair_rows, pair_rows), pair_rows)
+        dl, dz = k // ord_count, k % ord_count
+        owner = (la + dl) % lat_count * ord_count + (oz + dz) % ord_count
+        theirs = (owner * slots + g * GROUP) * 2
+        order = rows_ref[pl.ds(pl.multiple_of(theirs, pair_rows), pair_rows), :1]
+        shape = (pair_rows, lon_count)
+        part = (lax.broadcasted_iota(jnp.int32, shape, 0) % 2).astype(jnp.float32)
+        longitude = lax.broadcasted_iota(jnp.int32, shape, 1).astype(jnp.float32)
+        values = cosine(order * longitude + part * (lon_count // 4), lon_count)
+        table_ref[here, :] = (values * (1.0 / math.sqrt(lon_count))).astype(jnp.bfloat16)
+
+    def forward_step(t, carry):
+        g = t // tiles
+
+        @pl.when(t % tiles == 0)
+        def _():
+            def per_device(k, carry):
+                table_block(g, k)
+                return carry
+
+            lax.fori_loop(0, devices, per_device, 0)
+
+        table_rows = pl.ds(pl.multiple_of(g * devices * pair_rows, devices * pair_rows), devices * pair_rows)
+        tile = t % tiles
+        slot = t % 2
+
+        @pl.when(t + 1 < groups * tiles)
+        def _():
+            for c in x_copies((t + 1) % tiles, (t + 1) % 2):
+                c.start()
+
+        for c in x_copies(tile, slot):
+            c.wait()
+
+        def block(kb, carry):
+            rows = xv[slot, pl.ds(kb * BLOCK, BLOCK)].reshape(BLOCK * lanes, lon_count)
+            res = lax.dot_general(
+                table_ref[table_rows, :], rows, (((1,), (1,)), ((), ())), preferred_element_type=jnp.float32
+            )
+            for k in range(BLOCK):
+                piece = res[:, k * lanes : (k + 1) * lanes].reshape(devices, pair_rows, lanes)
+                stage[:, kb * BLOCK + k] = piece.astype(jnp.bfloat16)
+            return carry
+
+        lax.fori_loop(0, TILE // BLOCK, block, 0)
+        here = pl.ds(tile * TILE, TILE)
+        c0 = pltpu.make_async_copy(stage, fs_ref.at[g, :, here], stage_sem.at[0])
+        c1 = pltpu.make_async_copy(stage.at[0], cb_ref.at[g, 0, here], stage_sem.at[1])
+        c0.start()
+        c1.start()
+        c0.wait()
+        c1.wait()
+
+        for first, count in ((0, 1), (1, 1), (2, tiles - 2)):
+
+            @pl.when(t == first + count - 1)
+            def _():
+                ready = pl.ds(first * TILE, count * TILE)
+                for dl, dz in sends:
+                    part = (0, dl * ord_count + dz, ready)
+                    send(fs_ref, cb_ref, part, ahead(dl, dz), send_f.at[0], recv_f.at[0])
+
+        @pl.when(t == 2 * tiles - 1)
+        def _():
+            send_forward(1)
+
+        return carry
+
+    lax.fori_loop(0, groups * tiles, forward_step, 0)
+
+    def drain(ref, g, sem):
+        far = ref.at[g, pl.ds(1, devices - 1)]
+        pltpu.make_async_copy(far, far, sem).wait()
+
+    lane = lax.broadcasted_iota(jnp.int32, (half, lanes), 1)
+    low = lane < channels
+    places = [(a, b) for a in range(lat_count) for b in range(ord_count)]
+
+    def index_of(a, b):
+        return (la + (lat_count - a)) % lat_count * ord_count + (oz + (ord_count - b)) % ord_count
+
+    def slot_step(g, s):
+        q = g * GROUP + s
+        cur = q % 2
+
+        @pl.when(q + 1 < slots)
+        def _():
+            leg_copy(q + 1, (q + 1) % 2).start()
+
+        combos = [(p, t, a) for p in range(2) for t in range(ord_count // 2) for a in range(lat_count)]
+        for p, t, a in combos:
+            line = pl.ds(2 * s + p, half, stride=pair_rows)
+            first = z[a * ord_count + 2 * t, line, :]
+            second = z[a * ord_count + 2 * t + 1, line, :]
+            at = slice(p * width + t * lanes, p * width + (t + 1) * lanes)
+            rhs[a * 2 * half : a * 2 * half + half, at] = jnp.where(
+                low, first, pltpu.roll(second, channels, 1)
+            )
+            rhs[a * 2 * half + half : (a + 1) * 2 * half, at] = jnp.where(
+                low, pltpu.roll(first, channels, 1), second
+            )
+
+        leg_copy(q, cur).wait()
+        order = rows_ref[pl.ds(2 * (first_slot + q), 1), :1]
+        weight = 1.0 + jnp.minimum(order, 1.0)
+        gain = gains[...]
+        for k in reversed(range(order_bits)):
+            shift = 1 << k
+            bit = jnp.floor(order * (1.0 / shift)) - 2.0 * jnp.floor(order * (0.5 / shift))
+            if shift >= 8:
+                size = degrees + 8 + shift - 8
+                gain = jnp.where(bit > 0.5, gain[shift : shift + size], gain[:size])
+            else:
+                gain = jnp.where(bit > 0.5, pltpu.roll(gain, gain.shape[0] - shift, 0), gain)
+        gain = gain[:degrees]
+        for p in range(2):
+            at = slice(p * width, (p + 1) * width)
+            spec = jnp.dot(legv[cur], rhs[:, at].astype(jnp.bfloat16), preferred_element_type=jnp.float32)
+            filtered = (spec * gain).astype(jnp.bfloat16)
+            mixed = jnp.dot(filtered, mixing_ref[...], preferred_element_type=jnp.float32)
+            synth = lax.dot_general(
+                legv[cur], mixed.astype(jnp.bfloat16), (((0,), (0,)), ((), ())),
+                preferred_element_type=jnp.float32,
+            )
+            rhs[:, at] = synth * weight
+
+        for p, t, a in combos:
+            line = pl.ds(2 * s + p, half, stride=pair_rows)
+            at = slice(p * width + t * lanes, p * width + (t + 1) * lanes)
+            first = rhs[a * 2 * half : a * 2 * half + half, at]
+            second = rhs[a * 2 * half + half : (a + 1) * 2 * half, at]
+            z[a * ord_count + 2 * t, line, :] = jnp.where(low, first, pltpu.roll(second, channels, 1))
+            z[a * ord_count + 2 * t + 1, line, :] = jnp.where(
+                low, pltpu.roll(first, channels, 1), second
+            )
+
+    def middle_step(g, carry):
+        drain(cb_ref, g, recv_f.at[g])
+
+        @pl.when(g + 2 < groups)
+        def _():
+            send_forward(g + 2)
+
+        @pl.when(g == groups - 2)
+        def _():
+            send_back(0)
+
+        @pl.when(g == groups - 1)
+        def _():
+            for early in range(1, groups - 2):
+                send_back(early)
+
+        loads = [
+            pltpu.make_async_copy(cb_ref.at[g, index_of(a, b)], av.at[j], a_sem.at[j])
+            for j, (a, b) in enumerate(places)
+        ]
+        for c in loads:
+            c.start()
+        for c in loads:
+            c.wait()
+
+        def widen(j, carry):
+            z[j] = av[j].reshape(half * pair_rows, lanes).astype(jnp.float32)
+            return carry
+
+        lax.fori_loop(0, devices, widen, 0)
+
+        def per_slot(s, carry):
+            slot_step(g, s)
+            return carry
+
+        lax.fori_loop(0, GROUP, per_slot, 0)
+
+        def narrow(j, carry):
+            av[j] = z[j].reshape(half, pair_rows, lanes).astype(jnp.bfloat16)
+            return carry
+
+        lax.fori_loop(0, devices, narrow, 0)
+        stores = [
+            pltpu.make_async_copy(av.at[j], ys_ref.at[g, index_of(a, b)], a_sem.at[j])
+            for j, (a, b) in enumerate(places)
+        ]
+        own = pltpu.make_async_copy(av.at[la * ord_count + oz], yb_ref.at[g, 0], own_sem)
+        for c in stores:
+            c.start()
+        own.start()
+        for c in stores:
+            c.wait()
+        own.wait()
+
+        @pl.when(g == groups - 1)
+        def _():
+            for k, (first, count) in enumerate(cuts):
+                for late in (groups - 2, groups - 1):
+                    for dl, dz in sends:
+                        part = (late, dl * ord_count + dz, pl.ds(first * TILE, count * TILE))
+                        send(ys_ref, yb_ref, part, behind(dl, dz), send_r.at[late], recv_last.at[k])
+
+        return carry
+
+    gain_copy.wait()
+    lax.fori_loop(0, groups, middle_step, 0)
+
+    for c in x_copies(0, 0):
+        c.start()
+    for g in range(groups - 2):
+        drain(yb_ref, g, recv_r.at[g])
+
+    def out_copies(c, slot):
+        return [
+            pltpu.make_async_copy(
+                xv.at[slot, :, h], out_ref.at[pl.ds(h * half + c * TILE, TILE)], o_sem.at[slot, h]
+            )
+            for h in range(2)
+        ]
+
+    def inverse_step(c, carry):
+        slot = c % 2
+        for k, (first, count) in enumerate(cuts):
+
+            @pl.when(c == first)
+            def _():
+                rows_here = pl.ds(first * TILE, count * TILE)
+                far = yb_ref.at[pl.ds(groups - 2, 2), pl.ds(1, devices - 1), rows_here]
+                pltpu.make_async_copy(far, far, recv_last.at[k]).wait()
+
+        loads = [
+            pltpu.make_async_copy(
+                yb_ref.at[:, :, c * TILE + k], v.at[:, :, :, pl.ds(k * lanes, lanes)], v_sem.at[k]
+            )
+            for k in range(TILE)
+        ]
+        for copy in loads:
+            copy.start()
+
+        @pl.when(c >= 1)
+        def _():
+            for copy in out_copies(c - 1, 1 - slot):
+                copy.wait()
+
+        @pl.when(c + 1 < tiles)
+        def _():
+            for copy in x_copies(c + 1, 1 - slot):
+                copy.start()
+
+        for copy in x_copies(c, slot):
+            copy.wait()
+        for copy in loads:
+            copy.wait()
+        wide = BLOCK * lanes
+        depth = groups * devices * pair_rows
+
+        def block(kb, carry):
+            cols = pl.ds(pl.multiple_of(kb * wide, wide), wide)
+            back = lax.dot_general(
+                v[:, :, :, cols].reshape(depth, wide),
+                table_ref[...],
+                (((0,), (0,)), ((), ())),
+                preferred_element_type=jnp.float32,
+            )
+            here = pl.ds(kb * BLOCK, BLOCK)
+            state = xv[slot, here].reshape(wide, lon_count).astype(jnp.float32)
+            new = (state + jax.nn.gelu(back, approximate=True)).astype(jnp.bfloat16)
+            xv[slot, here] = new.reshape(BLOCK, 2, channels, lon_count)
+            return carry
+
+        lax.fori_loop(0, TILE // BLOCK, block, 0)
+        for copy in out_copies(c, slot):
+            copy.start()
+        return carry
+
+    lax.fori_loop(0, tiles, inverse_step, 0)
+    for copy in out_copies(tiles - 1, (tiles - 1) % 2):
+        copy.wait()
+    for g in range(groups):
+        drain(fs_ref, g, send_f.at[g])
+        drain(ys_ref, g, send_r.at[g])
+
+
+def fast_shards(state_field, slot_order, legendre, degree_gain, mixing):
+    channels, lat_rows, lon_count = state_field.shape
+    slots, degrees, latitudes = legendre.shape
+    width = mixing.shape[0]
+    lat_count = lax.axis_size("lat")
+    ord_count = lax.axis_size("ord")
+    devices = lat_count * ord_count
+    groups = slots // GROUP
+    half = lat_rows // 2
+    lanes = 2 * channels
+    pair_rows = 2 * GROUP
+    x = state_field.transpose(1, 0, 2)
+    rows = jnp.broadcast_to(jnp.repeat(slot_order, 2)[:, None], (2 * devices * slots, 128)).astype(jnp.float32)
+    order_bits = (devices * slots - 1).bit_length()
+    sizes = (lat_count, ord_count, groups, half, channels, slots)
+    buffer = jax.ShapeDtypeStruct((groups, devices, half, pair_rows, lanes), jnp.bfloat16)
+    tiles = half // TILE
+    anywhere = pl.BlockSpec(memory_space=pl.ANY)
+    vmem = pl.BlockSpec(memory_space=pltpu.VMEM)
+    sem = pltpu.SemaphoreType.DMA
+    flops = 4 * devices * slots * channels * lat_rows * lon_count
+    flops += 4 * slots * width * degrees * (2 * latitudes + width)
+    outs = pl.pallas_call(
+        functools.partial(whole_kernel, sizes),
+        out_shape=[jax.ShapeDtypeStruct(x.shape, jnp.bfloat16)] + [buffer] * 4,
+        in_specs=[anywhere, vmem, anywhere, anywhere, vmem],
+        out_specs=[anywhere] * 5,
+        scratch_shapes=[
+            pltpu.VMEM((groups * devices * pair_rows, lon_count), jnp.bfloat16),
+            pltpu.VMEM((degrees + (1 << order_bits), width), jnp.float32),
+            pltpu.VMEM((2, TILE, 2, channels, lon_count), jnp.bfloat16),
+            pltpu.VMEM((devices, TILE, pair_rows, lanes), jnp.bfloat16),
+            pltpu.VMEM((devices, half, pair_rows, lanes), jnp.bfloat16),
+            pltpu.VMEM((devices, half * pair_rows, lanes), jnp.float32),
+            pltpu.VMEM((2, degrees, latitudes), jnp.bfloat16),
+            pltpu.VMEM((latitudes, 2 * width), jnp.float32),
+            pltpu.VMEM((groups, devices, pair_rows, TILE * lanes), jnp.bfloat16),
+            sem,
+            sem((2, 2)),
+            sem((2,)),
+            sem((devices,)),
+            sem((2,)),
+            sem((TILE,)),
+            sem((2, 2)),
+            sem,
+            sem((groups,)),
+            sem((groups,)),
+            sem((groups,)),
+            sem((groups,)),
+            sem((len(cuts_of(tiles)),)),
+        ],
+        compiler_params=pltpu.CompilerParams(
+            collective_id=0, has_side_effects=True, vmem_limit_bytes=58 * 1024 * 1024
+        ),
+        cost_estimate=pl.CostEstimate(flops=flops, bytes_accessed=10**9, transcendentals=0),
+    )(x, rows, legendre, degree_gain, mixing)
+    return outs[0].transpose(1, 0, 2)
+
+
+def fits(mesh, state_field, legendre, mixing):
+    lat_count, ord_count = mesh.shape["lat"], mesh.shape["ord"]
+    channels = mixing.shape[0] // ord_count
+    lat_rows = state_field.shape[1] // lat_count
+    slots = legendre.shape[0] // (lat_count * ord_count)
+    return (
+        2 * channels == 128
+        and ord_count % 2 == 0
+        and lat_rows % (2 * TILE) == 0
+        and lat_rows // (2 * TILE) > 2
+        and slots % GROUP == 0
+        and slots // GROUP > 2
+        and state_field.shape[2] % 4 == 0
+    )
+
+
 def solution(mesh):
     placed = (P(("batch", "ord"), "lat", None), P(), P(("lat", "ord"), None, None), P(), P())
-    return jax.shard_map(
-        shards,
-        mesh=mesh,
-        in_specs=placed,
-        out_specs=P(("batch", "ord"), "lat", None),
-        check_vma=False,
-    )
+
+    def run(state_field, slot_order, legendre, degree_gain, mixing):
+        shards = fast_shards if fits(mesh, state_field, legendre, mixing) else plain_shards
+        return jax.shard_map(
+            shards,
+            mesh=mesh,
+            in_specs=placed,
+            out_specs=P(("batch", "ord"), "lat", None),
+            check_vma=False,
+        )(state_field, slot_order, legendre, degree_gain, mixing)
+
+    return run

time: 1310 us -> 1100 us (0.84)
  Pallas kernels: 87.5 us -> 1070 us
  local copies, waits for them, and re-layouts: 490 us -> 24.8 us
  waiting for transfers between devices: 365 us -> 0 us
  blocking collectives: 136 us -> 0 us
  matrix products: 118 us -> 0 us
  other arithmetic: 59.4 us -> 0.68 us
  starting transfers between devices: 40.6 us -> 0 us
    pallas_call x4 -> x1, Pallas kernels: 87.5 us -> 1070 us  [fast_shards(): pl.pallas_call(functools.partial(whole_kernel, sizes), out_shape=[jax.Sha...]
    all_to_all x7 -> x0, waiting for transfers between devices: 365 us -> none  [the longest x4 358 us: shards(): lax.all_to_all(fourier.reshape(devices, 2 * piece, rows), ('lat', 'ord'),...]
    reshape x21 -> x0, local copies, waits for them, and re-layouts: 359 us -> none  [the longest x8 162 us: shards(): coeffs.transpose(3, 2, 0, 4, 1, 5).reshape(piece, 2, latitudes, width)]
    all_to_all x1 -> x0, blocking collectives: 136 us -> none  [shards(): lax.all_to_all(outgoing, ('lat', 'ord'), split_axis=0, concat_axis=0, til...]
    dot_general x5 -> x0, matrix products: 118 us -> none  [the longest x4 72.9 us: shards(): lax.dot_general(rows_here, grid_rows, (((1,), (1,)), ((), ())), preferred...]
    transpose x4 -> x0, local copies, waits for them, and re-layouts: 75.6 us -> none  [shards(): outgoing.transpose(2, 4, 1, 0, 3, 5).reshape(devices, 2 * piece, rows)]
    convert_element_type x5 -> x1, other arithmetic: 59 us -> 0.68 us  [fast_shards(): jnp.broadcast_to(jnp.repeat(slot_order, 2)[:, None], (2 * devices * slots...]
    all_to_all x7 -> x0, starting transfers between devices: 40.6 us -> none  [the longest x4 22.4 us: shards(): lax.all_to_all(fourier.reshape(devices, 2 * piece, rows), ('lat', 'ord'),...]
  transfers between devices with their start and end apart: 7 -> 0, of which waited for: 6 -> 0; matrix products, arithmetic and copies ran while one was open for 41% -> 0% of each run, Pallas kernels for 7% -> 0%
where the time goes in v1:
time: 1100 us; the launch traced here: 1090 us
  Pallas kernels  1070 us (97%)
  local copies, waits for them, and re-layouts  24.8 us (2%)
    pallas_call x1, Pallas kernels, fast_shards(): pl.pallas_call(functools.partial(whole_kernel, sizes), out_shape=[jax.Sha...  1070 us
    unnamed x1, local copies, waits for them, and re-layouts  23.5 us

profile of v1, /device:TPU:0, one launch (start us, length us, event | category | flops | bytes accessed | tf_op | source)
XLA Modules:
  0.0 1092.1 jit_solution(1046313072713919845)
XLA Ops:
  0.0 0.7 convert_element_type.5
  0.7 0.1 broadcast_in_dim.8
  0.8 0.2 convert_element_type.6
  1.0 1.0 broadcast_in_dim.9.rows_ref
  2.0 1066.7 %shard_map.55 = (bf16[180,64,1440]{2,1,0:T(8,128)(2,1)}, bf16[4,16,90,16,128]{4,3,2,1,0:T(8,128)(2,1)}, bf16[4,16,90,16,128]{4,3,2,1,0:T(8,128)(2,1)}, bf16[4,16...) custom-call(bf16[180,64,1440]{2,1,0:T(8,128)(2,1)} %bitcast.3, f32[1024,128]{1,0:T(8,128)} %broadcast_in_dim.9.rows_ref, ...), custom_call_target="tpu_custom_call" | custom-call | flops 73987522560 | bytes 1000000000 | tf_op jit(solution)/shard_map/pallas_call | solution.py:530
  1068.7 23.5 %copy.7 = bf16[64,180,1440]{2,0,1:T(8,128)(2,1)} copy(bf16[64,180,1440]{2,0,1:T(8,128)(2,1)} %bitcast.2) | data formatting | bytes 66355200

commit v2 on v1

--- a/solution.py
+++ b/solution.py
@@ -132,7 +132,7 @@
 
 MESH = pl.DeviceIdType.MESH
 GROUP = 8
-TILE = 15
+TILE = 10
 BLOCK = 5
 
 
@@ -142,7 +142,9 @@
 
 
 def cuts_of(tiles):
-    counts = [2] * ((tiles - 2) // 2) + [1] * (tiles % 2 + 2)
+    counts = []
+    while sum(counts) < tiles:
+        counts.insert(0, min(len(counts) // 2 + 1, tiles - sum(counts)))
     return [(sum(counts[:k]), count) for k, count in enumerate(counts)]
 
 
@@ -279,7 +281,7 @@
         c0.wait()
         c1.wait()
 
-        for first, count in ((0, 1), (1, 1), (2, tiles - 2)):
+        for first, count in ((0, 1), (1, 2), (3, 3), (6, tiles - 6)):
 
             @pl.when(t == first + count - 1)
             def _():
@@ -573,7 +575,7 @@
         2 * channels == 128
         and ord_count % 2 == 0
         and lat_rows % (2 * TILE) == 0
-        and lat_rows // (2 * TILE) > 2
+        and lat_rows // (2 * TILE) > 6
         and slots % GROUP == 0
         and slots // GROUP > 2
         and state_field.shape[2] % 4 == 0

time: 1100 us -> 1070 us (0.973)
  Pallas kernels: 1070 us -> 1040 us
    pallas_call x1, Pallas kernels: 1070 us -> 1040 us  [fast_shards(): pl.pallas_call(functools.partial(whole_kernel, sizes), out_shape=[jax.Sha...]
where the time goes in v2:
time: 1070 us; the launch traced here: 1060 us
  Pallas kernels  1040 us (97%)
  local copies, waits for them, and re-layouts  24.8 us (2%)
    pallas_call x1, Pallas kernels, fast_shards(): pl.pallas_call(functools.partial(whole_kernel, sizes), out_shape=[jax.Sha...  1040 us
    unnamed x1, local copies, waits for them, and re-layouts  23.5 us

profile of v2, /device:TPU:0, one launch (start us, length us, event | category | flops | bytes accessed | tf_op | source)
XLA Modules:
  0.0 1064.6 jit_solution(14340385772566919247)
XLA Ops:
  0.0 0.7 convert_element_type.5
  0.7 0.1 broadcast_in_dim.8
  0.8 0.2 convert_element_type.6
  1.0 1.0 broadcast_in_dim.9.rows_ref
  2.0 1039.1 %shard_map.55 = (bf16[180,64,1440]{2,1,0:T(8,128)(2,1)}, bf16[4,16,90,16,128]{4,3,2,1,0:T(8,128)(2,1)}, bf16[4,16,90,16,128]{4,3,2,1,0:T(8,128)(2,1)}, bf16[4,16...) custom-call(bf16[180,64,1440]{2,1,0:T(8,128)(2,1)} %bitcast.3, f32[1024,128]{1,0:T(8,128)} %broadcast_in_dim.9.rows_ref, ...), custom_call_target="tpu_custom_call" | custom-call | flops 73987522560 | bytes 1000000000 | tf_op jit(solution)/shard_map/pallas_call | solution.py:532
  1041.1 23.5 %copy.7 = bf16[64,180,1440]{2,0,1:T(8,128)(2,1)} copy(bf16[64,180,1440]{2,0,1:T(8,128)(2,1)} %bitcast.2) | data formatting | bytes 66355200
